TPU v7x, 32 devices: a whole 2x2x4 slice. The times are simulated.
32 devices in a mesh: freq: 8 (over z, core), cell: 4 (over y, x).
Axes of the slice: x: 2, y: 2, z: 4, core: 2. Of those that a mesh axis runs over, the one named last changes fastest.
Arguments:
- covariance: bfloat16 [256, 2, 256, 256], P('freq', None, 'cell'), may hold values from -4 to 6, as said below
- replica: bfloat16 [256, 2, 256, 2048], P('freq', None, None, 'cell'), may hold values from -0.25 to 0.25
- transmission: bfloat16 [256, 2048], P('freq', 'cell'), may hold values from 0.29882812 to 3
Outputs:
- ambiguity: float32 [2048], P('cell')
- relative: float32 [2048], P('cell')
Inputs may be any that keep to these rules, and one draw needn't show every extreme that they name: Each covariance[f, 0] + i covariance[f, 1] is exactly Hermitian, also after rounding to bfloat16; before rounding all its eigenvalues are at least 0.5.
All inputs are finite; a program needn't handle non-finite values.
Results may differ from a plain program's by a relative error of at most 0.0003.
Values may be sent and summed in bfloat16 or wider, within the bound.
A program may use at most 384 MiB of HBM per device.

v0:
```python
import jax
import jax.numpy as jnp
from jax import lax
from jax.sharding import PartitionSpec as P


def quadratic(cov_piece, col_fields, row_fields):
    count, _, rows, depths = cov_piece.shape
    stacked = cov_piece.reshape(count, 2 * rows, depths)
    first = jnp.einsum(
        "fij,fjc->fic", stacked, col_fields[:, 0], preferred_element_type=jnp.float32
    )
    second = jnp.einsum(
        "fij,fjc->fic", stacked, col_fields[:, 1], preferred_element_type=jnp.float32
    )
    image_re = first[:, :rows] - second[:, rows:]
    image_im = first[:, rows:] + second[:, :rows]
    return jnp.sum(row_fields[:, 0] * image_re + row_fields[:, 1] * image_im, axis=1)


def shards(covariance, replica, transmission):
    freq_total = covariance.shape[0] * lax.axis_size("freq")
    power = quadratic(lax.all_gather(covariance, "cell", axis=2, tiled=True), replica, replica)
    amplitude = transmission.astype(jnp.float32)
    partial_value = jnp.sum(amplitude * amplitude * power, axis=0)
    partial_value = partial_value / jnp.float32(freq_total)
    ambiguity = lax.psum(partial_value, "freq")
    peak = lax.pmax(jnp.max(ambiguity), "cell")
    relative = ambiguity / jnp.maximum(peak, jnp.float32(1.0))
    return (ambiguity, relative)


def solution(mesh):
    return jax.shard_map(
        shards,
        mesh=mesh,
        in_specs=(P("freq", None, "cell", None), P("freq", None, None, "cell"), P("freq", "cell")),
        out_specs=(P("cell"), P("cell")),
        check_vma=False,
    )
```

profile of v0, /device:TPU:0, one launch (start us, length us, event | category | flops | bytes accessed | tf_op | source)
XLA Modules:
  0.0 197.6 jit_solution(6672672013921874193)
XLA Ops:
  7.2 0.0 all-gather.2.cloned.1.call-start
  7.2 0.7 all-gather.2.cloned.1.call-update
  7.9 92.2 %all-gather.2.cloned.1.call-done = bf16[32,2,256,256]{3,2,1,0:T(8,128)(2,1)} async-done(((bf16[32,2,64,256]{3,2,1,0:T(8,128)(2,1)}), bf16[32,2,256,256]{3,2,1,0:T(8,128)(2,1)}) %all-gather.2.cloned.1.call-update) | async-done | bytes 8388624 | tf_op jit(solution)/shard_map/all_gather | solution.py:23
  100.1 17.7 %fusion.4 = f32[32,512,512]{2,1,0:T(8,128)} fusion(bf16[32,512,256]{2,1,0:T(8,128)(2,1)} %bitcast.15, bf16[32,2,256,512]{3,2,1,0:T(8,128)(2,1)} %param.4), kind=kOutput, calls=%fused_computation.6 | convolution fusion | flops 4294967296 | bytes 50331648 | tf_op jit(solution)/shard_map/fij,fjc->fic/dot_general | solution.py:13
  117.8 17.7 %fusion.6 = f32[32,512,512]{2,1,0:T(8,128)} fusion(bf16[32,512,256]{2,1,0:T(8,128)(2,1)} %bitcast.16, bf16[32,2,256,512]{3,2,1,0:T(8,128)(2,1)} %param.4), kind=kOutput, calls=%fused_computation.8 | convolution fusion | flops 4294967296 | bytes 50331648 | tf_op jit(solution)/shard_map/fij,fjc->fic/dot_general | solution.py:10
  135.5 0.0 copy-start
  135.5 27.6 %fusion.2 = f32[32,512]{1,0:T(8,128)S(1)} fusion(f32[32,512,512]{2,1,0:T(8,128)} %fusion.4, f32[32,512,512]{2,1,0:T(8,128)} %fusion.6, bf16[32,2,256,512]{3,2,1,0:T(8,128)(2,1)} %param.4), kind=kLoop, calls=%fused_computation.3 | loop fusion | flops 33538048 | bytes 83951616 | tf_op jit(solution)/shard_map/reduce_sum | solution.py:18
  163.1 0.0 copy-done
  163.2 16.2 %psum.7 = f32[512]{0:T(512)S(1)} all-reduce(f32[512]{0:T(512)S(1)} %broadcast_multiply_fusion), channel_id=1, replica_groups=mesh['freq'=8,'cell'=4] {'freq'}, use_global_device_ids=true, to_apply=%region_2.0 | all-reduce | flops 512 | bytes 4096 | tf_op jit(solution)/shard_map/psum | solution.py:27
  179.4 0.0 copy-start.1
  179.4 0.6 reduce_max.9
  180.0 9.5 %pmax.7 = f32[]{:T(128)} all-reduce(f32[]{:T(128)} %reduce_max.9), channel_id=1, replica_groups=mesh['freq'=8,'cell'=4] {'cell'}, use_global_device_ids=true, to_apply=%region_4.0 | all-reduce | flops 1 | bytes 8 | tf_op jit(solution)/shard_map/pmax | solution.py:28
  190.2 0.6 broadcast_divide_fusion
  190.8 0.0 copy-done.1
  (2 shorter events, 0.0 us)
Async XLA Ops:
  7.2 92.9 %all-gather.2.cloned.1.call-start = ((), (), s32[]{:S(2)}) async-start(), calls=%async_computation | async-start | bytes 10485760 | tf_op jit(solution)/shard_map/all_gather | solution.py:23
  135.5 27.6 %copy-start = (bf16[32,512]{1,0:T(8,128)(2,1)S(1)}, bf16[32,512]{1,0:T(8,128)(2,1)}, u32[]{:S(2)}) copy-start(bf16[32,512]{1,0:T(8,128)(2,1)} %param.5) | copy-start | bytes 98308
  179.4 11.4 %copy-start.1 = (f32[512]{0:T(512)}, f32[512]{0:T(512)S(1)}, u32[]{:S(2)}) copy-start(f32[512]{0:T(512)S(1)} %psum.7) | copy-start | bytes 6148
Sparse Core Ops, SparseCore 0:
  9.8 90.1 all-gather.1
where the time goes:
time: 198 us
  waiting for transfers between devices  92.8 us (47%)
  matrix products  35.5 us (18%)
  other arithmetic  28.8 us (15%)
  blocking collectives  25.7 us (13%)
  between operations  14.7 us (7%)
    all_gather x1, waiting for transfers between devices, shards(): lax.all_gather(covariance, 'cell', axis=2, tiled=True)  92.2 us
    reduce_sum x1, other arithmetic, quadratic(): jnp.sum(row_fields[:, 0] * image_re + row_fields[:, 1] * image_im, axis=1)  27.6 us
    dot_general x1, matrix products, quadratic(): jnp.einsum('fij,fjc->fic', stacked, col_fields[:, 1], preferred_element_t...  17.7 us
    dot_general x1, matrix products, quadratic(): jnp.einsum('fij,fjc->fic', stacked, col_fields[:, 0], preferred_element_t...  17.7 us
    psum x1, blocking collectives, shards(): ambiguity = lax.psum(partial_value, 'freq')  16.2 us
    pmax x1, blocking collectives, shards(): peak = lax.pmax(jnp.max(ambiguity), 'cell')  9.54 us
  transfers between devices with their start and end apart: 1, of which 1 were waited for; matrix products, arithmetic and copies ran while one was open for 0% of the time, Pallas kernels for 0%

commit v1 on v0

--- a/solution.py
+++ b/solution.py
@@ -1,7 +1,13 @@
+import functools
+
 import jax
 import jax.numpy as jnp
 from jax import lax
+from jax.experimental import pallas as pl
+from jax.experimental.pallas import tpu as pltpu
 from jax.sharding import PartitionSpec as P
+
+MESH = pl.DeviceIdType.MESH
 
 
 def quadratic(cov_piece, col_fields, row_fields):
@@ -18,7 +24,7 @@
     return jnp.sum(row_fields[:, 0] * image_re + row_fields[:, 1] * image_im, axis=1)
 
 
-def shards(covariance, replica, transmission):
+def plain(covariance, replica, transmission):
     freq_total = covariance.shape[0] * lax.axis_size("freq")
     power = quadratic(lax.all_gather(covariance, "cell", axis=2, tiled=True), replica, replica)
     amplitude = transmission.astype(jnp.float32)
@@ -30,7 +36,304 @@
     return (ambiguity, relative)
 
 
+def turned(z):
+    half = z.shape[1] // 2
+    return jnp.concatenate([z[:, half:], z[:, :half]], axis=1)
+
+
+def kernel(
+    freqs, group, cov_hbm, rep_hbm, trans_ref, amb_ref, rel_ref,
+    cov, v, sx, sy, rx, ry, rd, s0, s1, masks, amp, acc, gath, peaks,
+    cov_sem, rep_sem, send_sem, recv_sem, gsend, grecv, msend, mrecv,
+):
+    count, _, rows, depths = cov_hbm.shape
+    groups = count // group
+    pairs = group // 2
+    cells = rep_hbm.shape[2]
+    wide = 2 * rows
+    fme = lax.axis_index("freq")
+    me = lax.axis_index("cell")
+    y = me // 2
+    x = me % 2
+    at_x = 2 * y + (1 - x)
+    at_y = 2 * (1 - y) + x
+    at_d = 2 * (1 - y) + (1 - x)
+    partners = (at_x, at_y, at_d)
+
+    def cov_copy(g):
+        span = pl.ds(g * group, group)
+        return pltpu.make_async_copy(cov_hbm.at[span], cov.at[span], cov_sem.at[g])
+
+    def rep_copy(g):
+        span = pl.ds(g * group, group)
+        return pltpu.make_async_copy(rep_hbm.at[span], v.at[span], rep_sem.at[g])
+
+    for g in range(groups):
+        cov_copy(g).start()
+    for g in range(groups):
+        rep_copy(g).start()
+
+    barrier = pltpu.get_barrier_semaphore()
+    for partner in partners:
+        pl.semaphore_signal(barrier, inc=1, device_id={"cell": partner}, device_id_type=MESH)
+    for k in range(1, freqs):
+        other = (fme + k) % freqs
+        pl.semaphore_signal(barrier, inc=1, device_id={"freq": other}, device_id_type=MESH)
+
+    def remote(g, which):
+        span = pl.ds(g * pairs, pairs)
+        if which == 0:
+            source, target = sx.at[span], rx.at[span]
+        elif which == 1:
+            source, target = sy.at[span], ry.at[span]
+        else:
+            source, target = sx.at[span, 3], rd.at[span]
+        return pltpu.make_async_remote_copy(
+            src_ref=source,
+            dst_ref=target,
+            send_sem=send_sem.at[which, g],
+            recv_sem=recv_sem.at[which, g],
+            device_id={"cell": partners[which]},
+            device_id_type=MESH,
+        )
+
+    row = lax.broadcasted_iota(jnp.int32, (rows, wide), 0)
+    lane = lax.broadcasted_iota(jnp.int32, (rows, wide), 1)
+
+    def triangle(col):
+        inside = jnp.logical_and(col >= 0, col < rows)
+        upper = jnp.where(col > row, 1.0, jnp.where(col == row, 0.5, 0.0))
+        lower = jnp.where(col < row, 1.0, 0.0)
+        zero = jnp.zeros((rows, wide), jnp.float32)
+        full = jnp.where(inside, 1.0, zero)
+        return full, jnp.where(inside, upper, zero), jnp.where(inside, lower, zero)
+
+    own_set = triangle(lane - rows * x)
+    oth_set = triangle(lane - rows * (1 - x))
+    made = (
+        own_set[0], oth_set[0], own_set[0] - own_set[2], own_set[2], oth_set[1], oth_set[2],
+        own_set[1] + oth_set[0], own_set[2] + oth_set[0],
+    )
+    for k, mask in enumerate(made):
+        masks[k] = mask.astype(jnp.bfloat16)
+    amplitude = trans_ref[...].astype(jnp.float32)
+    amp[...] = amplitude * amplitude
+    s0[...] = jnp.zeros_like(s0)
+    s1[...] = jnp.zeros_like(s1)
+    acc[...] = jnp.zeros_like(acc)
+
+    own_tile = pl.ds(pl.multiple_of(y * wide, wide), wide)
+    opp_tile = pl.ds(pl.multiple_of((1 - y) * wide, wide), wide)
+
+    def pack(p):
+        own, oth = masks[0], masks[1]
+        up, low = masks[2], masks[3]
+        f0, f1 = 2 * p, 2 * p + 1
+        a0, b0 = cov[f0, 0, :, own_tile], cov[f0, 1, :, own_tile]
+        a1, b1 = cov[f1, 0, :, own_tile], cov[f1, 1, :, own_tile]
+        c0, d0 = cov[f0, 0, :, opp_tile], cov[f0, 1, :, opp_tile]
+        c1, d1 = cov[f1, 0, :, opp_tile], cov[f1, 1, :, opp_tile]
+        p0 = a0 * up + b0 * low
+        p1 = a1 * up + b1 * low
+        sy[p, 0] = p0 + a0 * oth
+        sy[p, 1] = p1 + a1 * oth
+        sy[p, 2] = turned(b0 * oth) + b1 * oth
+        sy[p, 3] = turned(c1 * oth) + d1 * oth
+        sx[p, 0] = c0
+        sx[p, 1] = d0
+        sx[p, 2] = c1 * own + turned(d1 * own)
+        sx[p, 3] = p0 + turned(p1)
+
+    def pack_group(g):
+        cov_copy(g).wait()
+        for k in range(pairs):
+            pack(g * pairs + k)
+
+    def send_group(g):
+        for which in range(3):
+            remote(g, which).start()
+
+    pack_group(0)
+    pl.semaphore_wait(barrier, len(partners) + freqs - 1)
+
+    def ahead(g, carry):
+        pack_group(g)
+        send_group(g - 1)
+        return carry
+
+    lax.fori_loop(1, groups, ahead, 0)
+    send_group(groups - 1)
+
+    def put(s, block, own_side, ta, tb):
+        base = pl.multiple_of(block * rows, rows)
+        tile = y if own_side else 1 - y
+        first = pl.ds(base, rows)
+        second = pl.ds(pl.multiple_of(depths + base, rows), rows)
+        left = pl.ds(pl.multiple_of(tile * wide, wide), wide)
+        right = pl.ds(pl.multiple_of(depths + tile * wide, wide), wide)
+        s[first, left] = ta
+        s[first, right] = -tb
+        s[second, left] = tb
+        s[second, right] = ta
+
+    def build(p):
+        own, oth = masks[0], masks[1]
+        own_low = masks[3]
+        oth_up, oth_low = masks[4], masks[5]
+        own_up_oth, own_low_oth = masks[6], masks[7]
+        f0, f1 = 2 * p, 2 * p + 1
+        for f, s in ((f0, s0), (f1, s1)):
+            put(s, me, True, cov[f, 0, :, own_tile] * own_up_oth, cov[f, 1, :, own_tile] * own_low_oth)
+            put(s, me, False, cov[f, 0, :, opp_tile], cov[f, 1, :, opp_tile])
+        diag = rx[p, 3]
+        put(s0, at_x, True, diag * oth_up, diag * oth_low)
+        put(s0, at_x, False, rx[p, 0], rx[p, 1])
+        diag = turned(diag)
+        put(s1, at_x, True, diag * oth_up, diag * oth_low)
+        block = rx[p, 2]
+        put(s1, at_x, False, block * oth, turned(block * own))
+        b_both = ry[p, 2]
+        block = ry[p, 0]
+        put(s0, at_y, False, block * own_up_oth, block * own_low + turned(b_both * own))
+        block = ry[p, 1]
+        put(s1, at_y, False, block * own_up_oth, block * own_low + b_both * oth)
+        block = ry[p, 3]
+        put(s1, at_y, True, turned(block * own), block * oth)
+        diag = rd[p]
+        put(s0, at_d, False, diag * oth_up, diag * oth_low)
+        diag = turned(diag)
+        put(s1, at_d, False, diag * oth_up, diag * oth_low)
+
+    part = 256 if cells % 256 == 0 else cells
+
+    def apply(f, s):
+        for c in range(0, cells, part):
+            field = v[f, :, c:c + part]
+            image = jnp.dot(s[...], field, preferred_element_type=jnp.float32)
+            product = image * field.astype(jnp.float32)
+            folded = jnp.sum(product.reshape(2 * depths // 8, 8, part), axis=0)
+            acc[:, c:c + part] += folded * amp[pl.ds(f, 1), c:c + part]
+
+    def step(g, carry):
+        rep_copy(g).wait()
+        for which in range(3):
+            remote(g, which).wait_recv()
+
+        def pair(k, inner):
+            p = g * pairs + k
+            build(p)
+            apply(2 * p, s0)
+            apply(2 * p + 1, s1)
+            return inner
+
+        return lax.fori_loop(0, pairs, pair, carry)
+
+    lax.fori_loop(0, groups, step, 0)
+
+    scale = 2.0 / (count * freqs)
+    gath[fme] = jnp.sum(acc[...], axis=0, keepdims=True) * scale
+
+    def drain(g, carry):
+        for which in range(3):
+            remote(g, which).wait_send()
+        return carry
+
+    lax.fori_loop(0, groups, drain, 0)
+
+    def share(k):
+        other = (fme + k) % freqs
+        return pltpu.make_async_remote_copy(
+            src_ref=gath.at[fme], dst_ref=gath.at[fme],
+            send_sem=gsend.at[k], recv_sem=grecv.at[k],
+            device_id={"freq": other}, device_id_type=MESH,
+        )
+
+    for k in range(1, freqs):
+        share(k).start()
+    for k in range(1, freqs):
+        share(k).wait_recv()
+    total = gath[0]
+    for k in range(1, freqs):
+        total = total + gath[k]
+    amb_ref[...] = total
+    top = jnp.max(total, axis=1, keepdims=True)
+    peaks[3] = jnp.broadcast_to(top, (1, 128))
+    sent = []
+    for k, partner in enumerate(partners):
+        copy = pltpu.make_async_remote_copy(
+            src_ref=peaks.at[3], dst_ref=peaks.at[k],
+            send_sem=msend.at[k], recv_sem=mrecv.at[k],
+            device_id={"cell": partner}, device_id_type=MESH,
+        )
+        copy.start()
+        sent.append(copy)
+    for k in range(1, freqs):
+        share(k).wait_send()
+    for copy in sent:
+        copy.wait()
+    best = jnp.max(jnp.max(peaks[...], axis=0), axis=1, keepdims=True)
+    rel_ref[...] = total / jnp.maximum(best, 1.0)
+
+
+def fused(freqs, group, covariance, replica, transmission):
+    count, _, rows, depths = covariance.shape
+    cells = replica.shape[3]
+    fields = replica.reshape(count, 2 * depths, cells)
+    groups = count // group
+    wide = 2 * rows
+    bf, f32 = jnp.bfloat16, jnp.float32
+    dma = pltpu.SemaphoreType.DMA
+    vm = pltpu.VMEM
+    amb, rel = pl.pallas_call(
+        functools.partial(kernel, freqs, group),
+        out_shape=[jax.ShapeDtypeStruct((1, cells), f32)] * 2,
+        in_specs=[
+            pl.BlockSpec(memory_space=pl.ANY),
+            pl.BlockSpec(memory_space=pl.ANY),
+            pl.BlockSpec(memory_space=pltpu.VMEM),
+        ],
+        out_specs=[pl.BlockSpec(memory_space=pltpu.VMEM)] * 2,
+        scratch_shapes=[
+            vm((count, 2, rows, depths), bf),
+            vm((count, 2 * depths, cells), bf),
+            vm((count // 2, 4, rows, wide), bf),
+            vm((count // 2, 4, rows, wide), bf),
+            vm((count // 2, 4, rows, wide), bf),
+            vm((count // 2, 4, rows, wide), bf),
+            vm((count // 2, rows, wide), bf),
+            vm((2 * depths, 2 * depths), bf),
+            vm((2 * depths, 2 * depths), bf),
+            vm((8, rows, wide), bf),
+            vm((count, cells), f32),
+            vm((8, cells), f32),
+            vm((freqs, 1, cells), f32),
+            vm((4, 1, 128), f32),
+            dma((groups,)),
+            dma((groups,)),
+            dma((3, groups)),
+            dma((3, groups)),
+            dma((freqs,)),
+            dma((freqs,)),
+            dma((3,)),
+            dma((3,)),
+        ],
+        compiler_params=pltpu.CompilerParams(
+            collective_id=0, has_side_effects=True, vmem_limit_bytes=60 * 1024 * 1024
+        ),
+    )(covariance, fields, transmission)
+    return amb.reshape(cells), rel.reshape(cells)
+
+
 def solution(mesh):
+    freqs = mesh.shape["freq"]
+    four = mesh.shape["cell"] == 4
+
+    def shards(covariance, replica, transmission):
+        count, _, rows, _ = covariance.shape
+        if four and freqs > 1 and rows == 64 and count % 4 == 0 and replica.shape[3] % 128 == 0:
+            return fused(freqs, 4, covariance, replica, transmission)
+        return plain(covariance, replica, transmission)
+
     return jax.shard_map(
         shards,
         mesh=mesh,

time: 198 us -> 49.6 us (0.25)
  waiting for transfers between devices: 92.8 us -> 0 us
  Pallas kernels: 0 us -> 46.2 us
  matrix products: 35.5 us -> 0 us
  other arithmetic: 28.8 us -> 0 us
  blocking collectives: 25.7 us -> 0 us
  between operations: 14.7 us -> 0.64 us
  local copies, waits for them, and re-layouts: 0.01 us -> 2.48 us
    all_gather x1 -> x0, waiting for transfers between devices: 92.2 us -> none  [shards(): lax.all_gather(covariance, 'cell', axis=2, tiled=True)]
    pallas_call x0 -> x1, Pallas kernels: none -> 46.2 us  [fused(): pl.pallas_call(functools.partial(kernel, freqs, group), out_shape=[jax.Sh...]
    dot_general x2 -> x0, matrix products: 35.5 us -> none  [the longest x1 17.7 us: quadratic(): jnp.einsum('fij,fjc->fic', stacked, col_fields[:, 1], preferred_element_t...]
    reduce_sum x2 -> x0, other arithmetic: 27.6 us -> none  [the longest x1 27.6 us: quadratic(): jnp.sum(row_fields[:, 0] * image_re + row_fields[:, 1] * image_im, axis=1)]
    psum x1 -> x0, blocking collectives: 16.2 us -> none  [shards(): ambiguity = lax.psum(partial_value, 'freq')]
    pmax x1 -> x0, blocking collectives: 9.54 us -> none  [shards(): peak = lax.pmax(jnp.max(ambiguity), 'cell')]
    unnamed x4 -> x2, local copies, waits for them, and re-layouts: 0.01 us -> 2.48 us
  transfers between devices with their start and end apart: 1 -> 0, of which waited for: 1 -> 0; matrix products, arithmetic and copies ran while one was open for 0% -> 0% of each run, Pallas kernels for 0% -> 0%
where the time goes in v1:
time: 49.6 us; the launch traced here: 49.3 us
  Pallas kernels  46.2 us (93%)
  local copies, waits for them, and re-layouts  2.48 us (5%)
  between operations  0.64 us (1%)
    pallas_call x1, Pallas kernels, fused(): pl.pallas_call(functools.partial(kernel, freqs, group), out_shape=[jax.Sh...  46.2 us
    unnamed x2, local copies, waits for them, and re-layouts  2.48 us

profile of v1, /device:TPU:0, one launch (start us, length us, event | category | flops | bytes accessed | tf_op | source)
XLA Modules:
  0.0 49.3 jit_solution(8079751718962305577)
XLA Ops:
  0.6 46.2 %shard_map.50 = (f32[1,512]{1,0:T(1,128)}, f32[1,512]{1,0:T(1,128)}) custom-call(bf16[32,2,64,256]{3,2,1,0:T(8,128)(2,1)} %cov_hbm.1, bf16[32,512,512]{2,1,0:T(8,128)(2,1)} %bitcast.3, bf16[32,512]{1,0:T(8,128)(2,1)} %trans_ref.1), custom_call_target="tpu_custom_call" | custom-call | tf_op jit(solution)/shard_map/pallas_call | solution.py:287
  46.9 1.2 %copy.7 = f32[512]{0:T(512)} copy(f32[512]{0:T(512)} %bitcast.5) | data formatting | bytes 4096
  48.1 1.2 %copy.8 = f32[512]{0:T(512)} copy(f32[512]{0:T(512)} %bitcast.4) | data formatting | bytes 4096

commit v2 on v1

--- a/solution.py
+++ b/solution.py
@@ -86,14 +86,16 @@
             source, target = sx.at[span], rx.at[span]
         elif which == 1:
             source, target = sy.at[span], ry.at[span]
+        elif which == 2:
+            source, target = rx.at[g * pairs, 3], rd.at[g * pairs]
         else:
-            source, target = sx.at[span, 3], rd.at[span]
+            source, target = ry.at[g * pairs + 1, 0], rd.at[g * pairs + 1]
         return pltpu.make_async_remote_copy(
             src_ref=source,
             dst_ref=target,
             send_sem=send_sem.at[which, g],
             recv_sem=recv_sem.at[which, g],
-            device_id={"cell": partners[which]},
+            device_id={"cell": at_x if which in (0, 3) else at_y},
             device_id_type=MESH,
         )
 
@@ -112,7 +114,7 @@
     oth_set = triangle(lane - rows * (1 - x))
     made = (
         own_set[0], oth_set[0], own_set[0] - own_set[2], own_set[2], oth_set[1], oth_set[2],
-        own_set[1] + oth_set[0], own_set[2] + oth_set[0],
+        own_set[1] + oth_set[0], own_set[2] + oth_set[0], own_set[1],
     )
     for k, mask in enumerate(made):
         masks[k] = mask.astype(jnp.bfloat16)
@@ -135,14 +137,15 @@
         c1, d1 = cov[f1, 0, :, opp_tile], cov[f1, 1, :, opp_tile]
         p0 = a0 * up + b0 * low
         p1 = a1 * up + b1 * low
-        sy[p, 0] = p0 + a0 * oth
-        sy[p, 1] = p1 + a1 * oth
+        diag = p0 + turned(p1)
+        sy[p, 0] = diag
+        sy[p, 1] = turned(a0 * oth) + a1 * oth
         sy[p, 2] = turned(b0 * oth) + b1 * oth
         sy[p, 3] = turned(c1 * oth) + d1 * oth
         sx[p, 0] = c0
         sx[p, 1] = d0
         sx[p, 2] = c1 * own + turned(d1 * own)
-        sx[p, 3] = p0 + turned(p1)
+        sx[p, 3] = diag
 
     def pack_group(g):
         cov_copy(g).wait()
@@ -150,19 +153,15 @@
             pack(g * pairs + k)
 
     def send_group(g):
-        for which in range(3):
+        for which in range(2):
             remote(g, which).start()
 
     pack_group(0)
     pl.semaphore_wait(barrier, len(partners) + freqs - 1)
-
-    def ahead(g, carry):
-        pack_group(g)
-        send_group(g - 1)
-        return carry
-
-    lax.fori_loop(1, groups, ahead, 0)
-    send_group(groups - 1)
+    pack_group(1)
+    send_group(0)
+    pack_group(2)
+    send_group(1)
 
     def put(s, block, own_side, ta, tb):
         base = pl.multiple_of(block * rows, rows)
@@ -192,11 +191,12 @@
         put(s1, at_x, True, diag * oth_up, diag * oth_low)
         block = rx[p, 2]
         put(s1, at_x, False, block * oth, turned(block * own))
-        b_both = ry[p, 2]
-        block = ry[p, 0]
-        put(s0, at_y, False, block * own_up_oth, block * own_low + turned(b_both * own))
-        block = ry[p, 1]
-        put(s1, at_y, False, block * own_up_oth, block * own_low + b_both * oth)
+        own_up = masks[8]
+        a_both, b_both = ry[p, 1], ry[p, 2]
+        diag = ry[p, 0]
+        put(s0, at_y, False, diag * own_up + turned(a_both * own), diag * own_low + turned(b_both * own))
+        diag = turned(diag)
+        put(s1, at_y, False, diag * own_up + a_both * oth, diag * own_low + b_both * oth)
         block = ry[p, 3]
         put(s1, at_y, True, turned(block * own), block * oth)
         diag = rd[p]
@@ -214,10 +214,10 @@
             folded = jnp.sum(product.reshape(2 * depths // 8, 8, part), axis=0)
             acc[:, c:c + part] += folded * amp[pl.ds(f, 1), c:c + part]
 
-    def step(g, carry):
+    def work(g):
         rep_copy(g).wait()
-        for which in range(3):
-            remote(g, which).wait_recv()
+        remote(g, 2).wait_recv()
+        remote(g, 3).wait_recv()
 
         def pair(k, inner):
             p = g * pairs + k
@@ -226,15 +226,39 @@
             apply(2 * p + 1, s1)
             return inner
 
-        return lax.fori_loop(0, pairs, pair, carry)
+        lax.fori_loop(0, pairs, pair, 0)
+
+    def pass_on(g):
+        remote(g, 0).wait_recv()
+        remote(g, 2).start()
+        remote(g, 1).wait_recv()
+        remote(g, 3).start()
+
+    def step(g, carry):
+        pass_on(g)
+
+        @pl.when(g + 2 < groups)
+        def _():
+            send_group(g + 2)
+
+        @pl.when(g + 3 < groups)
+        def _():
+            pack_group(g + 3)
+
+        @pl.when(g > 0)
+        def _():
+            work(g - 1)
+
+        return carry
 
     lax.fori_loop(0, groups, step, 0)
+    work(groups - 1)
 
     scale = 2.0 / (count * freqs)
     gath[fme] = jnp.sum(acc[...], axis=0, keepdims=True) * scale
 
     def drain(g, carry):
-        for which in range(3):
+        for which in range(4):
             remote(g, which).wait_send()
         return carry
 
@@ -303,15 +327,15 @@
             vm((count // 2, rows, wide), bf),
             vm((2 * depths, 2 * depths), bf),
             vm((2 * depths, 2 * depths), bf),
-            vm((8, rows, wide), bf),
+            vm((9, rows, wide), bf),
             vm((count, cells), f32),
             vm((8, cells), f32),
             vm((freqs, 1, cells), f32),
             vm((4, 1, 128), f32),
             dma((groups,)),
             dma((groups,)),
-            dma((3, groups)),
-            dma((3, groups)),
+            dma((4, groups)),
+            dma((4, groups)),
             dma((freqs,)),
             dma((freqs,)),
             dma((3,)),
@@ -330,7 +354,7 @@
 
     def shards(covariance, replica, transmission):
         count, _, rows, _ = covariance.shape
-        if four and freqs > 1 and rows == 64 and count % 4 == 0 and replica.shape[3] % 128 == 0:
+        if four and freqs > 1 and rows == 64 and count % 4 == 0 and count >= 12 and replica.shape[3] % 128 == 0:
             return fused(freqs, 4, covariance, replica, transmission)
         return plain(covariance, replica, transmission)
 

time: 49.6 us -> 49.1 us (0.990)
  no operation moved by 1% of the time
where the time goes in v2:
time: 49.1 us; the launch traced here: 48.9 us
  Pallas kernels  45.8 us (93%)
  local copies, waits for them, and re-layouts  2.48 us (5%)
  between operations  0.64 us (1%)
    pallas_call x1, Pallas kernels, fused(): pl.pallas_call(functools.partial(kernel, freqs, group), out_shape=[jax.Sh...  45.8 us
    unnamed x2, local copies, waits for them, and re-layouts  2.48 us

profile of v2, /device:TPU:0, one launch (start us, length us, event | category | flops | bytes accessed | tf_op | source)
XLA Modules:
  0.0 48.9 jit_solution(1271534403133290763)
XLA Ops:
  0.6 45.8 %shard_map.50 = (f32[1,512]{1,0:T(1,128)}, f32[1,512]{1,0:T(1,128)}) custom-call(bf16[32,2,64,256]{3,2,1,0:T(8,128)(2,1)} %cov_hbm.1, bf16[32,512,512]{2,1,0:T(8,128)(2,1)} %bitcast.3, bf16[32,512]{1,0:T(8,128)(2,1)} %trans_ref.1), custom_call_target="tpu_custom_call" | custom-call | tf_op jit(solution)/shard_map/pallas_call | solution.py:311
  46.4 1.2 %copy.7 = f32[512]{0:T(512)} copy(f32[512]{0:T(512)} %bitcast.5) | data formatting | bytes 4096
  47.7 1.2 %copy.8 = f32[512]{0:T(512)} copy(f32[512]{0:T(512)} %bitcast.4) | data formatting | bytes 4096
